TPU v7x, 32 devices: a whole 2x2x4 slice. The times are simulated.
32 devices in a mesh: gx: 8 (over y, x, core), gy: 4 (over z).
Axes of the slice: x: 2, y: 2, z: 4, core: 2. Of those that a mesh axis runs over, the one named last changes fastest.
Arguments:
- field: float32 [65536, 512], P(('gx', 'gy')), may hold values from -6 to 6
Outputs:
- spectrum: float32 [65536, 512], P('gx', 'gy')
All inputs are finite; a program needn't handle non-finite values.
Results may differ from a plain program's by a relative error of at most 0.00007.
Values sent between devices are 32-bit elements; how exact they have to be, the bound alone decides.
A program may use at most 64 MiB of HBM per device.

v0:
```python
import math
import jax
import jax.numpy as jnp
from jax import lax
from jax.sharding import PartitionSpec as P

P_SIZE = 256
Q = 256
highest = lax.Precision.HIGHEST


def mat_dot(left, right):
    return jnp.dot(left, right, precision=highest, preferred_element_type=jnp.float32)


def finish(spec_real, spec_imag, frequency):
    length = P_SIZE * Q
    phases = math.pi / (2.0 * length) * frequency.astype(jnp.float32)
    factor = math.sqrt(2.0 / length)
    return factor * (
        jnp.cos(phases)[:, :, None] * spec_real + jnp.sin(phases)[:, :, None] * spec_imag
    )


def body(field):
    groups = lax.axis_size("gx")
    position = lax.axis_index("gx")
    length = P_SIZE * Q
    joined = lax.all_to_all(field, "gy", split_axis=1, concat_axis=0, tiled=True)
    row_count = joined.shape[0]
    col_width = joined.shape[1]
    half_rows = P_SIZE // (2 * groups)
    local_q = Q // groups
    local_p = P_SIZE // groups
    paired = joined.reshape(row_count // 2, 2, col_width)
    even_rows = paired[:, 0].reshape(half_rows, Q, col_width)
    odd_rows = jnp.flip(paired[:, 1].reshape(half_rows, Q, col_width), axis=1)
    low_half, high_half = (
        lax.all_to_all(even_rows, "gx", split_axis=1, concat_axis=0, tiled=True),
        lax.all_to_all(odd_rows, "gx", split_axis=1, concat_axis=0, tiled=True),
    )
    freq_first = jnp.arange(P_SIZE, dtype=jnp.int32)
    place_low = jnp.arange(P_SIZE // 2, dtype=jnp.int32)
    place_high = P_SIZE - 1 - place_low
    two_pi = 2.0 * math.pi
    low_phase = (
        two_pi / P_SIZE * (freq_first[:, None] * place_low[None, :] % P_SIZE).astype(jnp.float32)
    )
    high_phase = (
        two_pi / P_SIZE * (freq_first[:, None] * place_high[None, :] % P_SIZE).astype(jnp.float32)
    )
    flat_low = low_half.reshape(P_SIZE // 2, local_q * col_width)
    flat_high = high_half.reshape(P_SIZE // 2, local_q * col_width)
    cos_part = (
        mat_dot(jnp.cos(low_phase), flat_low) + mat_dot(jnp.cos(high_phase), flat_high)
    ).reshape(P_SIZE, local_q, col_width)
    sin_part = (
        mat_dot(jnp.sin(low_phase), flat_low) + mat_dot(jnp.sin(high_phase), flat_high)
    ).reshape(P_SIZE, local_q, col_width)
    part_imag = -sin_part
    second_place = position * local_q + jnp.arange(local_q, dtype=jnp.int32)
    turn_phase = (
        two_pi / length * (freq_first[:, None] * second_place[None, :] % length).astype(jnp.float32)
    )
    turn_cos = jnp.cos(turn_phase)[:, :, None]
    turn_sin = jnp.sin(turn_phase)[:, :, None]
    turned_real = cos_part * turn_cos + part_imag * turn_sin
    turned_imag = part_imag * turn_cos - cos_part * turn_sin
    moved_real, moved_imag = (
        lax.all_to_all(turned_real, "gx", split_axis=0, concat_axis=1, tiled=True),
        lax.all_to_all(turned_imag, "gx", split_axis=0, concat_axis=1, tiled=True),
    )
    second_index = jnp.arange(Q, dtype=jnp.int32)
    row_phase = two_pi / Q * (second_index[:, None] * second_index[None, :] % Q).astype(jnp.float32)
    row_cos = jnp.cos(row_phase)
    row_sin = jnp.sin(row_phase)
    spec_real = jnp.einsum("jb,kbc->jkc", row_cos, moved_real, precision=highest) + jnp.einsum(
        "jb,kbc->jkc", row_sin, moved_imag, precision=highest
    )
    spec_imag = jnp.einsum("jb,kbc->jkc", row_cos, moved_imag, precision=highest) - jnp.einsum(
        "jb,kbc->jkc", row_sin, moved_real, precision=highest
    )
    block_rows = lax.dynamic_slice_in_dim(freq_first, position * local_p, local_p, 0)
    frequency = block_rows[None, :] + P_SIZE * second_index[:, None]
    result = finish(spec_real, spec_imag, frequency)
    arrived = lax.all_to_all(result, "gx", split_axis=0, concat_axis=1, tiled=True)
    return arrived.reshape(local_q * P_SIZE, col_width)


def solution(mesh):
    in_specs = (P(("gx", "gy"), None),)
    out_specs = P("gx", "gy")
    return jax.shard_map(body, mesh=mesh, in_specs=in_specs, out_specs=out_specs, check_vma=False)
```

profile of v0, /device:TPU:0, one launch (start us, length us, event | category | flops | bytes accessed | tf_op | source)
XLA Modules:
  0.0 380.9 jit_solution(13258083812697321297)
XLA Ops:
  0.0 5.3 %copy.15 = f32[2048,512]{0,1:T(8,128)} copy(f32[2048,512]{1,0:T(8,128)} %param.1) | data formatting | bytes 8388608 | tf_op args[0]
  5.3 100.6 %all_to_all.97 = f32[2048,4,128]{0,2,1:T(8,128)} all-to-all(f32[2048,4,128]{0,2,1:T(8,128)} %bitcast.81), channel_id=1, replica_groups=mesh['gx'=8,'gy'=4] {'gy'}, dimensions={1} | all-to-all | bytes 8388608 | tf_op jit(solution)/shard_map/all_to_all | solution.py:29
  105.9 5.3 %copy.16 = f32[4,2048,128]{2,1,0:T(8,128)} copy(f32[4,2048,128]{1,2,0:T(8,128)} %bitcast.79) | data formatting | bytes 8388608 | tf_op jit(solution)/shard_map/all_to_all | solution.py:29
  111.2 7.7 %fusion.96 = (f32[4096,1,128]{2,1,0:T(1,128)}, f32[4096,1,128]{2,1,0:T(1,128)S(1)}) fusion(f32[4096,2,128]{2,1,0:T(2,128)} %bitcast.78), kind=kLoop, calls=%fused_computation.111 | loop fusion | bytes 8388608 | tf_op jit(solution)/shard_map/slice | solution.py:37
  118.9 2.5 copy.17
  121.4 3.8 all-to-all-start.1
  125.2 4.1 %copy.20 = f32[16,256,128]{2,0,1:T(8,128)} copy(f32[16,256,128]{2,1,0:T(8,128)} %bitcast.83) | data formatting | bytes 4194304 | tf_op jit(solution)/shard_map/reshape;squeeze | solution.py:37
  129.3 3.1 rev.4
  132.4 19.4 %all-to-all-done.1 = f32[16,256,128]{2,0,1:T(8,128)S(1)} async-done(((f32[16,256,128]{2,0,1:T(8,128)}), f32[16,256,128]{2,0,1:T(8,128)S(1)}, u32[]{:S(2)}, u32[]{:S(2)}) %all-to-all-start.1) | async-done | bytes 2097184 | tf_op jit(solution)/shard_map/all_to_all | solution.py:39
  151.8 4.9 %all-to-all-start.2 = ((f32[16,256,128]{2,0,1:T(8,128)}), f32[16,256,128]{2,0,1:T(8,128)}, u32[]{:S(2)}, u32[]{:S(2)}) async-start(f32[16,256,128]{2,0,1:T(8,128)} %rev.4), calls=%async_computation.2 | async-start | bytes 4194304 | tf_op jit(solution)/shard_map/all_to_all | solution.py:40
  156.7 0.5 fusion.57
  157.3 0.6 copy.19
  157.9 7.3 %fusion.9 = f32[256,4096]{1,0:T(8,128)} fusion(f32[16,8,32,128]{3,2,1,0:T(8,128)S(1)} %bitcast.73), kind=kOutput, calls=%fused_computation.16 | convolution fusion | flops 1611071488 | bytes 6291456 | tf_op jit(solution)/shard_map/dot_general | solution.py:13
  165.2 7.5 %fusion.7 = f32[256,4096]{1,0:T(8,128)} fusion(f32[16,8,32,128]{3,2,1,0:T(8,128)S(1)} %bitcast.74), kind=kOutput, calls=%fused_computation.14 | convolution fusion | flops 1611071488 | bytes 6291456 | tf_op jit(solution)/shard_map/dot_general | solution.py:13
  172.7 10.6 %all-to-all-done.2 = f32[16,256,128]{2,0,1:T(8,128)} async-done(((f32[16,256,128]{2,0,1:T(8,128)}), f32[16,256,128]{2,0,1:T(8,128)}, u32[]{:S(2)}, u32[]{:S(2)}) %all-to-all-start.2) | async-done | bytes 2097184 | tf_op jit(solution)/shard_map/all_to_all | solution.py:40
  183.3 0.0 copy-start.3
  183.3 2.4 copy.22
  185.7 0.4 copy-done.3
  186.1 4.9 %fusion.3 = f32[32,8,32,128]{3,1,2,0:T(8,128)S(1)} fusion(f32[256,4096]{1,0:T(8,128)S(1)} %copy-done.3, f32[16,8,32,128]{3,2,1,0:T(8,128)S(1)} %bitcast.75, s32[128]{0:T(128)S(1)} %iota_subtract_fusion), kind=kOutput, calls=%fused_computation.10 | convolution fusion | flops 1612120064 | bytes 10486272 | tf_op jit(solution)/shard_map/dot_general | solution.py:13
  191.1 0.0 copy-start.2
  191.1 0.8 copy.31
  191.9 1.4 copy-done.2
  193.3 5.0 %fusion.4 = f32[32,8,32,128]{3,1,2,0:T(8,128)S(1)} fusion(f32[256,4096]{1,0:T(8,128)S(1)} %copy-done.2, f32[16,8,32,128]{3,2,1,0:T(8,128)S(1)} %bitcast.76, s32[128]{0:T(128)S(1)} %iota_subtract_fusion), kind=kOutput, calls=%fused_computation.11 | convolution fusion | flops 1613168640 | bytes 10486272 | tf_op jit(solution)/shard_map/dot_general | solution.py:13
  198.2 1.0 copy.32
  199.2 4.6 %fusion.1 = (f32[256,32,128]{2,1,0:T(8,128)}, f32[256,32,128]{2,1,0:T(8,128)S(1)}) fusion(f32[32,8,32,128]{3,2,1,0:T(8,128)S(1)} %copy.32, f32[32,8,32,128]{3,2,1,0:T(8,128)S(1)} %copy.31, f32[256,32]{1,0:T(8,128)S(1)} %get-tuple-element.12, f32[256,32]{1,0:T(8,128)S(1)} %get-tuple-element.11), kind=kLoop, calls=%fused_computation.5 | loop fusion | flops 6291456 | bytes 16842752 | tf_op jit(solution)/shard_map/add | solution.py:67
  203.8 52.3 %all_to_all.98 = f32[256,32,128]{2,1,0:T(8,128)} all-to-all(f32[256,32,128]{2,1,0:T(8,128)S(1)} %get-tuple-element.6), channel_id=1, replica_groups=mesh['gx'=8,'gy'=4] {'gx'}, dimensions={0} | all-to-all | bytes 8388608 | tf_op jit(solution)/shard_map/all_to_all | solution.py:71
  256.1 4.6 %all-to-all-start.3 = ((f32[256,32,128]{2,1,0:T(8,128)}), f32[256,32,128]{2,1,0:T(8,128)}, u32[]{:S(2)}, u32[]{:S(2)}) async-start(f32[256,32,128]{2,1,0:T(8,128)} %get-tuple-element.5), calls=%async_computation.3 | async-start | bytes 8388608 | tf_op jit(solution)/shard_map/all_to_all | solution.py:70
  260.7 0.1 dynamic_slice.3
  260.8 0.2 fusion.63
  261.0 2.8 copy.24
  263.8 7.1 %fusion.19 = f32[256,32,128]{2,0,1:T(8,128)} fusion(f32[32,256,128]{2,1,0:T(8,128)S(1)} %bitcast.71), kind=kOutput, calls=%fused_computation.29 | convolution fusion | flops 3222142976 | bytes 8388608 | tf_op jit(solution)/shard_map/jb,kbc->jkc/dot_general | solution.py:77
  270.9 7.3 %fusion.21 = f32[256,32,128]{2,0,1:T(8,128)} fusion(f32[32,256,128]{2,1,0:T(8,128)S(1)} %bitcast.72), kind=kOutput, calls=%fused_computation.31 | convolution fusion | flops 3222142976 | bytes 8388608 | tf_op jit(solution)/shard_map/jb,kbc->jkc/dot_general | solution.py:80
  278.2 31.5 %all-to-all-done.3 = f32[256,32,128]{2,1,0:T(8,128)} async-done(((f32[256,32,128]{2,1,0:T(8,128)}), f32[256,32,128]{2,1,0:T(8,128)}, u32[]{:S(2)}, u32[]{:S(2)}) %all-to-all-start.3) | async-done | bytes 4194336 | tf_op jit(solution)/shard_map/all_to_all | solution.py:70
  309.8 2.8 copy.23
  312.6 0.0 copy-start
  312.6 0.0 copy-start.1
  312.6 4.8 %fusion.23 = f32[256,32,128]{2,0,1:T(8,128)S(1)} fusion(f32[32,256,128]{2,1,0:T(8,128)S(1)} %bitcast.69), kind=kOutput, calls=%fused_computation.33 | convolution fusion | flops 3222142976 | bytes 8388608 | tf_op jit(solution)/shard_map/jb,kbc->jkc/dot_general | solution.py:77
  317.4 0.0 copy-done
  317.4 0.0 copy-done.1
  317.4 6.1 %add_multiply_fusion = f32[256,32,128]{2,0,1:T(8,128)S(1)} fusion(f32[256,32,128]{2,0,1:T(8,128)S(1)} %copy-done.1, f32[256,32,128]{2,0,1:T(8,128)S(1)} %fusion.23, f32[256,32,128]{2,0,1:T(8,128)S(1)} %copy-done, f32[32,256,128]{2,1,0:T(8,128)S(1)} %bitcast.70, f32[256,32]{0,1:T(8,128)S(1)} %get-tuple-element.10, f32[256,32]{0,1:T(8,128)S(1)} %get-tuple-element.9), kind=kOutput, calls=%fused_computation.9 | convolution fusion | flops 3228434432 | bytes 21037056 | tf_op jit(solution)/shard_map/jb,kbc->jkc/dot_general | solution.py:80
  323.5 2.7 copy.25
  326.3 51.5 %all_to_all.99 = f32[256,32,128]{2,1,0:T(8,128)S(1)} all-to-all(f32[256,32,128]{2,1,0:T(8,128)S(1)} %copy.25), channel_id=1, replica_groups=mesh['gx'=8,'gy'=4] {'gx'}, dimensions={0} | all-to-all | bytes 8388608 | tf_op jit(solution)/shard_map/all_to_all | solution.py:86
  377.8 2.7 copy.26
  (4 shorter events, 0.0 us)
Async XLA Ops:
  121.4 30.4 %all-to-all-start.1 = ((f32[16,256,128]{2,0,1:T(8,128)}), f32[16,256,128]{2,0,1:T(8,128)S(1)}, u32[]{:S(2)}, u32[]{:S(2)}) async-start(f32[16,256,128]{2,0,1:T(8,128)} %copy.17), calls=%async_computation.1 | async-start | bytes 4194304 | tf_op jit(solution)/shard_map/all_to_all | solution.py:39
  151.8 31.5 %all-to-all-start.2 = ((f32[16,256,128]{2,0,1:T(8,128)}), f32[16,256,128]{2,0,1:T(8,128)}, u32[]{:S(2)}, u32[]{:S(2)}) async-start(f32[16,256,128]{2,0,1:T(8,128)} %rev.4), calls=%async_computation.2 | async-start | bytes 4194304 | tf_op jit(solution)/shard_map/all_to_all | solution.py:40
  183.3 2.8 copy-start.3
  191.1 2.2 copy-start.2
  256.1 53.7 %all-to-all-start.3 = ((f32[256,32,128]{2,1,0:T(8,128)}), f32[256,32,128]{2,1,0:T(8,128)}, u32[]{:S(2)}, u32[]{:S(2)}) async-start(f32[256,32,128]{2,1,0:T(8,128)} %get-tuple-element.5), calls=%async_computation.3 | async-start | bytes 8388608 | tf_op jit(solution)/shard_map/all_to_all | solution.py:70
  312.6 4.8 %copy-start = (f32[256,32,128]{2,0,1:T(8,128)S(1)}, f32[256,32,128]{2,0,1:T(8,128)}, u32[]{:S(2)}) copy-start(f32[256,32,128]{2,0,1:T(8,128)} %fusion.19) | copy-start | bytes 12582916
  312.6 4.8 %copy-start.1 = (f32[256,32,128]{2,0,1:T(8,128)S(1)}, f32[256,32,128]{2,0,1:T(8,128)}, u32[]{:S(2)}) copy-start(f32[256,32,128]{2,0,1:T(8,128)} %fusion.21) | copy-start | bytes 12582916
where the time goes:
time: 386 us; the launch traced here: 381 us
  blocking collectives  204 us (53%)
  waiting for transfers between devices  61.6 us (16%)
  matrix products  50 us (13%)
  local copies, waits for them, and re-layouts  45.8 us (12%)
  starting transfers between devices  13.2 us (3%)
  other arithmetic  5.36 us (1%)
    all_to_all x1, blocking collectives, body(): lax.all_to_all(field, 'gy', split_axis=1, concat_axis=0, tiled=True)  101 us
    all_to_all x1, blocking collectives, body(): lax.all_to_all(turned_imag, 'gx', split_axis=0, concat_axis=1, tiled=True)  52.3 us
    all_to_all x1, blocking collectives, body(): lax.all_to_all(result, 'gx', split_axis=0, concat_axis=1, tiled=True)  51.5 us
    all_to_all x1, waiting for transfers between devices, body(): lax.all_to_all(turned_real, 'gx', split_axis=0, concat_axis=1, tiled=True)  31.5 us
    dot_general x4, matrix products, mat_dot(): jnp.dot(left, right, precision=highest, preferred_element_type=jnp.float32)  24.7 us
    all_to_all x1, waiting for transfers between devices, body(): lax.all_to_all(even_rows, 'gx', split_axis=1, concat_axis=0, tiled=True)  19.4 us
    all_to_all x1, waiting for transfers between devices, body(): lax.all_to_all(odd_rows, 'gx', split_axis=1, concat_axis=0, tiled=True)  10.6 us
    unnamed x11, local copies, waits for them, and re-layouts  8.93 us
  transfers between devices with their start and end apart: 3, of which 3 were waited for; matrix products, arithmetic and copies ran while one was open for 11% of the time, Pallas kernels for 0%

commit v1 on v0

--- a/solution.py
+++ b/solution.py
@@ -67,7 +67,12 @@
     turned_real = cos_part * turn_cos + part_imag * turn_sin
     turned_imag = part_imag * turn_cos - cos_part * turn_sin
     moved_real, moved_imag = (
-        lax.all_to_all(turned_real, "gx", split_axis=0, concat_axis=1, tiled=True),
+        jnp.concatenate(
+            lax.all_to_all(
+                jnp.stack(jnp.split(turned_real, lax.axis_size("gx"), axis=0)), "gx", 0, 0
+            ),
+            axis=1,
+        ),
         lax.all_to_all(turned_imag, "gx", split_axis=0, concat_axis=1, tiled=True),
     )
     second_index = jnp.arange(Q, dtype=jnp.int32)

time: 386 us -> 388 us (level)
  blocking collectives: 204 us -> 152 us
  waiting for transfers between devices: 61.6 us -> 99.6 us
  local copies, waits for them, and re-layouts: 45.8 us -> 56.9 us
  starting transfers between devices: 13.2 us -> 17.7 us
    all_to_all x1 -> x0, blocking collectives: 52.3 us -> none  [body(): lax.all_to_all(turned_imag, 'gx', split_axis=0, concat_axis=1, tiled=True)]
    all_to_all x1 -> x2, waiting for transfers between devices: 31.5 us -> 69.6 us  [the longest x1 38 us: body(): lax.all_to_all(turned_imag, 'gx', split_axis=0, concat_axis=1, tiled=True)]
    unnamed x11 -> x20, local copies, waits for them, and re-layouts: 8.93 us -> 19.2 us
    all_to_all x1 -> x2, starting transfers between devices: 4.55 us -> 9.11 us  [the longest x1 4.56 us: body(): lax.all_to_all(jnp.stack(jnp.split(turned_real, lax.axis_size('gx'), axis...]
  transfers between devices with their start and end apart: 3 -> 4, of which waited for: 3 -> 4; matrix products, arithmetic and copies ran while one was open for 11% -> 14% of each run, Pallas kernels for 0% -> 0%
where the time goes in v1:
time: 388 us; the launch traced here: 383 us
  blocking collectives  152 us (39%)
  waiting for transfers between devices  99.6 us (26%)
  local copies, waits for them, and re-layouts  56.9 us (15%)
  matrix products  50 us (13%)
  starting transfers between devices  17.7 us (5%)
  other arithmetic  6.11 us (2%)
    all_to_all x1, blocking collectives, body(): lax.all_to_all(field, 'gy', split_axis=1, concat_axis=0, tiled=True)  101 us
    all_to_all x1, blocking collectives, body(): lax.all_to_all(result, 'gx', split_axis=0, concat_axis=1, tiled=True)  51.5 us
    all_to_all x1, waiting for transfers between devices, body(): lax.all_to_all(turned_imag, 'gx', split_axis=0, concat_axis=1, tiled=True)  38 us
    all_to_all x1, waiting for transfers between devices, body(): lax.all_to_all(jnp.stack(jnp.split(turned_real, lax.axis_size('gx'), axis...  31.6 us
    dot_general x4, matrix products, mat_dot(): jnp.dot(left, right, precision=highest, preferred_element_type=jnp.float32)  24.7 us
    all_to_all x1, waiting for transfers between devices, body(): lax.all_to_all(even_rows, 'gx', split_axis=1, concat_axis=0, tiled=True)  19.4 us
    unnamed x20, local copies, waits for them, and re-layouts  19.2 us
    all_to_all x1, waiting for transfers between devices, body(): lax.all_to_all(odd_rows, 'gx', split_axis=1, concat_axis=0, tiled=True)  10.6 us
  transfers between devices with their start and end apart: 4, of which 4 were waited for; matrix products, arithmetic and copies ran while one was open for 14% of the time, Pallas kernels for 0%

profile of v1, /device:TPU:0, one launch (start us, length us, event | category | flops | bytes accessed | tf_op | source)
XLA Modules:
  0.0 383.1 jit_solution(1016363120658451150)
XLA Ops:
  0.0 5.3 %copy.15 = f32[2048,512]{0,1:T(8,128)} copy(f32[2048,512]{1,0:T(8,128)} %param.1) | data formatting | bytes 8388608 | tf_op args[0]
  5.3 100.6 %all_to_all.84 = f32[2048,4,128]{0,2,1:T(8,128)} all-to-all(f32[2048,4,128]{0,2,1:T(8,128)} %bitcast.110), channel_id=1, replica_groups=mesh['gx'=8,'gy'=4] {'gy'}, dimensions={1} | all-to-all | bytes 8388608 | tf_op jit(solution)/shard_map/all_to_all | solution.py:29
  105.9 5.3 %copy.16 = f32[4,2048,128]{2,1,0:T(8,128)} copy(f32[4,2048,128]{1,2,0:T(8,128)} %bitcast.108) | data formatting | bytes 8388608 | tf_op jit(solution)/shard_map/all_to_all | solution.py:29
  111.2 7.7 %fusion.104 = (f32[4096,1,128]{2,1,0:T(1,128)}, f32[4096,1,128]{2,1,0:T(1,128)S(1)}) fusion(f32[4096,2,128]{2,1,0:T(2,128)} %bitcast.107), kind=kLoop, calls=%fused_computation.127 | loop fusion | bytes 8388608 | tf_op jit(solution)/shard_map/slice | solution.py:37
  118.9 2.5 copy.17
  121.5 3.7 all-to-all-start.1
  125.2 4.1 %copy.20 = f32[16,256,128]{2,0,1:T(8,128)} copy(f32[16,256,128]{2,1,0:T(8,128)} %bitcast.112) | data formatting | bytes 4194304 | tf_op jit(solution)/shard_map/reshape;squeeze | solution.py:37
  129.3 3.1 rev.4
  132.4 19.4 %all-to-all-done.1 = f32[16,256,128]{2,0,1:T(8,128)S(1)} async-done(((f32[16,256,128]{2,0,1:T(8,128)}), f32[16,256,128]{2,0,1:T(8,128)S(1)}, u32[]{:S(2)}, u32[]{:S(2)}) %all-to-all-start.1) | async-done | bytes 2097184 | tf_op jit(solution)/shard_map/all_to_all | solution.py:39
  151.8 4.9 %all-to-all-start.2 = ((f32[16,256,128]{2,0,1:T(8,128)}), f32[16,256,128]{2,0,1:T(8,128)}, u32[]{:S(2)}, u32[]{:S(2)}) async-start(f32[16,256,128]{2,0,1:T(8,128)} %rev.4), calls=%async_computation.2 | async-start | bytes 4194304 | tf_op jit(solution)/shard_map/all_to_all | solution.py:40
  156.7 0.5 fusion.65
  157.3 0.6 copy.19
  157.9 7.3 %fusion.9 = f32[256,4096]{1,0:T(8,128)} fusion(f32[16,8,32,128]{3,2,1,0:T(8,128)S(1)} %bitcast.103), kind=kOutput, calls=%fused_computation.16 | convolution fusion | flops 1611071488 | bytes 6291456 | tf_op jit(solution)/shard_map/dot_general | solution.py:13
  165.2 7.5 %fusion.7 = f32[256,4096]{1,0:T(8,128)} fusion(f32[16,8,32,128]{3,2,1,0:T(8,128)S(1)} %bitcast.104), kind=kOutput, calls=%fused_computation.14 | convolution fusion | flops 1611071488 | bytes 6291456 | tf_op jit(solution)/shard_map/dot_general | solution.py:13
  172.7 10.6 %all-to-all-done.2 = f32[16,256,128]{2,0,1:T(8,128)} async-done(((f32[16,256,128]{2,0,1:T(8,128)}), f32[16,256,128]{2,0,1:T(8,128)}, u32[]{:S(2)}, u32[]{:S(2)}) %all-to-all-start.2) | async-done | bytes 2097184 | tf_op jit(solution)/shard_map/all_to_all | solution.py:40
  183.3 0.0 copy-start.4
  183.3 2.4 copy.22
  185.7 0.4 copy-done.4
  186.2 4.9 %fusion.3 = f32[32,8,32,128]{3,1,2,0:T(8,128)S(1)} fusion(f32[256,4096]{1,0:T(8,128)S(1)} %copy-done.4, f32[16,8,32,128]{3,2,1,0:T(8,128)S(1)} %bitcast.105, s32[128]{0:T(128)S(1)} %iota_subtract_fusion), kind=kOutput, calls=%fused_computation.10 | convolution fusion | flops 1612120064 | bytes 10486272 | tf_op jit(solution)/shard_map/dot_general | solution.py:13
  191.1 0.0 copy-start.3
  191.1 0.8 copy.31
  191.9 1.4 copy-done.3
  193.3 5.0 %fusion.4 = f32[32,8,32,128]{3,1,2,0:T(8,128)S(1)} fusion(f32[256,4096]{1,0:T(8,128)S(1)} %copy-done.3, f32[16,8,32,128]{3,2,1,0:T(8,128)S(1)} %bitcast.106, s32[128]{0:T(128)S(1)} %iota_subtract_fusion), kind=kOutput, calls=%fused_computation.11 | convolution fusion | flops 1613168640 | bytes 10486272 | tf_op jit(solution)/shard_map/dot_general | solution.py:13
  198.3 1.0 copy.32
  199.2 5.4 %fusion.1 = (f32[256,32,128]{2,1,0:T(8,128)}, f32[256,32,128]{2,1,0:T(8,128)}) fusion(f32[32,8,32,128]{3,2,1,0:T(8,128)S(1)} %copy.32, f32[32,8,32,128]{3,2,1,0:T(8,128)S(1)} %copy.31, f32[256,32]{1,0:T(8,128)S(1)} %get-tuple-element.12, f32[256,32]{1,0:T(8,128)S(1)} %get-tuple-element.11), kind=kLoop, calls=%fused_computation.5 | loop fusion | flops 6291456 | bytes 16842752 | tf_op jit(solution)/shard_map/add | solution.py:67
  204.6 4.5 %all-to-all-start.4 = ((f32[256,32,128]{2,1,0:T(8,128)}), f32[256,32,128]{2,1,0:T(8,128)}, u32[]{:S(2)}, u32[]{:S(2)}) async-start(f32[256,32,128]{2,1,0:T(8,128)} %get-tuple-element.6), calls=%async_computation.4 | async-start | bytes 8388608 | tf_op jit(solution)/shard_map/all_to_all | solution.py:76
  209.2 0.0 copy-start.2
  209.2 2.1 fusion.22
  211.2 1.9 fusion.21
  213.1 1.9 fusion.20
  215.0 1.9 fusion.19
  216.9 0.0 copy-done.2
  216.9 0.8 fusion.18
  217.7 0.8 fusion.17
  218.6 0.8 fusion.16
  219.4 0.8 fusion.15
  220.2 38.0 %all-to-all-done.4 = f32[256,32,128]{2,1,0:T(8,128)} async-done(((f32[256,32,128]{2,1,0:T(8,128)}), f32[256,32,128]{2,1,0:T(8,128)}, u32[]{:S(2)}, u32[]{:S(2)}) %all-to-all-start.4) | async-done | bytes 4194336 | tf_op jit(solution)/shard_map/all_to_all | solution.py:76
  258.2 4.6 %all-to-all-start.3 = ((f32[8,32,32,128]{3,2,1,0:T(8,128)}), f32[8,32,32,128]{3,2,1,0:T(8,128)}, u32[]{:S(2)}, u32[]{:S(2)}) async-start(f32[8,32,32,128]{3,2,1,0:T(8,128)} %fusion.15), calls=%async_computation.3 | async-start | bytes 8388608 | tf_op jit(solution)/shard_map/all_to_all | solution.py:71
  262.8 0.1 dynamic_slice.3
  262.9 0.2 fusion.71
  263.1 2.8 copy.24
  265.9 7.1 %fusion.27 = f32[256,32,128]{2,0,1:T(8,128)} fusion(f32[32,256,128]{2,1,0:T(8,128)S(1)} %bitcast.101), kind=kOutput, calls=%fused_computation.45 | convolution fusion | flops 3222142976 | bytes 8388608 | tf_op jit(solution)/shard_map/jb,kbc->jkc/dot_general | solution.py:82
  273.1 7.3 %fusion.29 = f32[256,32,128]{2,0,1:T(8,128)} fusion(f32[32,256,128]{2,1,0:T(8,128)S(1)} %bitcast.102), kind=kOutput, calls=%fused_computation.47 | convolution fusion | flops 3222142976 | bytes 8388608 | tf_op jit(solution)/shard_map/jb,kbc->jkc/dot_general | solution.py:85
  280.4 31.6 %all-to-all-done.3 = f32[8,32,32,128]{3,2,1,0:T(8,128)} async-done(((f32[8,32,32,128]{3,2,1,0:T(8,128)}), f32[8,32,32,128]{3,2,1,0:T(8,128)}, u32[]{:S(2)}, u32[]{:S(2)}) %all-to-all-start.3) | async-done | bytes 4194336 | tf_op jit(solution)/shard_map/all_to_all | solution.py:71
  311.9 2.8 copy.23
  314.7 0.0 copy-start
  314.8 0.0 copy-start.1
  314.8 4.8 %fusion.31 = f32[256,32,128]{2,0,1:T(8,128)S(1)} fusion(f32[32,256,128]{2,1,0:T(8,128)S(1)} %bitcast.99), kind=kOutput, calls=%fused_computation.49 | convolution fusion | flops 3222142976 | bytes 8388608 | tf_op jit(solution)/shard_map/jb,kbc->jkc/dot_general | solution.py:82
  319.5 0.0 copy-done
  319.5 0.0 copy-done.1
  319.5 6.1 %add_multiply_fusion = f32[256,32,128]{2,0,1:T(8,128)S(1)} fusion(f32[256,32,128]{2,0,1:T(8,128)S(1)} %copy-done.1, f32[256,32,128]{2,0,1:T(8,128)S(1)} %fusion.31, f32[256,32,128]{2,0,1:T(8,128)S(1)} %copy-done, f32[32,256,128]{2,1,0:T(8,128)S(1)} %bitcast.100, f32[256,32]{0,1:T(8,128)S(1)} %get-tuple-element.10, f32[256,32]{0,1:T(8,128)S(1)} %get-tuple-element.9), kind=kOutput, calls=%fused_computation.9 | convolution fusion | flops 3228434432 | bytes 21037056 | tf_op jit(solution)/shard_map/jb,kbc->jkc/dot_general | solution.py:85
  325.7 2.7 copy.25
  328.4 51.5 %all_to_all.85 = f32[256,32,128]{2,1,0:T(8,128)S(1)} all-to-all(f32[256,32,128]{2,1,0:T(8,128)S(1)} %copy.25), channel_id=1, replica_groups=mesh['gx'=8,'gy'=4] {'gx'}, dimensions={0} | all-to-all | bytes 8388608 | tf_op jit(solution)/shard_map/all_to_all | solution.py:91
  379.9 2.7 copy.26
  (4 shorter events, 0.0 us)
Async XLA Ops:
  121.5 30.4 %all-to-all-start.1 = ((f32[16,256,128]{2,0,1:T(8,128)}), f32[16,256,128]{2,0,1:T(8,128)S(1)}, u32[]{:S(2)}, u32[]{:S(2)}) async-start(f32[16,256,128]{2,0,1:T(8,128)} %copy.17), calls=%async_computation.1 | async-start | bytes 4194304 | tf_op jit(solution)/shard_map/all_to_all | solution.py:39
  151.8 31.5 %all-to-all-start.2 = ((f32[16,256,128]{2,0,1:T(8,128)}), f32[16,256,128]{2,0,1:T(8,128)}, u32[]{:S(2)}, u32[]{:S(2)}) async-start(f32[16,256,128]{2,0,1:T(8,128)} %rev.4), calls=%async_computation.2 | async-start | bytes 4194304 | tf_op jit(solution)/shard_map/all_to_all | solution.py:40
  183.3 2.8 copy-start.4
  191.1 2.2 copy-start.3
  204.6 53.7 %all-to-all-start.4 = ((f32[256,32,128]{2,1,0:T(8,128)}), f32[256,32,128]{2,1,0:T(8,128)}, u32[]{:S(2)}, u32[]{:S(2)}) async-start(f32[256,32,128]{2,1,0:T(8,128)} %get-tuple-element.6), calls=%async_computation.4 | async-start | bytes 8388608 | tf_op jit(solution)/shard_map/all_to_all | solution.py:76
  209.2 7.7 %copy-start.2 = (f32[256,32,128]{2,1,0:T(8,128)S(1)}, f32[256,32,128]{2,1,0:T(8,128)}, u32[]{:S(2)}) copy-start(f32[256,32,128]{2,1,0:T(8,128)} %get-tuple-element.5) | copy-start | bytes 12582916
  258.2 53.7 %all-to-all-start.3 = ((f32[8,32,32,128]{3,2,1,0:T(8,128)}), f32[8,32,32,128]{3,2,1,0:T(8,128)}, u32[]{:S(2)}, u32[]{:S(2)}) async-start(f32[8,32,32,128]{3,2,1,0:T(8,128)} %fusion.15), calls=%async_computation.3 | async-start | bytes 8388608 | tf_op jit(solution)/shard_map/all_to_all | solution.py:71
  314.7 4.8 %copy-start = (f32[256,32,128]{2,0,1:T(8,128)S(1)}, f32[256,32,128]{2,0,1:T(8,128)}, u32[]{:S(2)}) copy-start(f32[256,32,128]{2,0,1:T(8,128)} %fusion.27) | copy-start | bytes 12582916
  314.8 4.8 %copy-start.1 = (f32[256,32,128]{2,0,1:T(8,128)S(1)}, f32[256,32,128]{2,0,1:T(8,128)}, u32[]{:S(2)}) copy-start(f32[256,32,128]{2,0,1:T(8,128)} %fusion.29) | copy-start | bytes 12582916
